TPU v7x, 32 devices: a whole 2x2x4 slice. The times are simulated.
32 devices in a mesh: pert: 2 (over x), ga: 16 (over z, y, core).
Axes of the slice: x: 2, y: 2, z: 4, core: 2. Of those that a mesh axis runs over, the one named last changes fastest.
Arguments:
- psi_k: bfloat16 [2, 8192, 256], P(None, 'ga'), may hold values from -6 to 6
- beta_k: bfloat16 [2, 8192, 2496], P(None, 'ga'), may hold values from -0.0625 to 0.0625
- beta_kq: bfloat16 [2, 8192, 2496], P(None, 'ga'), may hold values from -0.15625 to 0.15625
- g_k: float32 [3, 8192], P(None, 'ga'), may hold values from -2 to 2
- g_kq: float32 [3, 8192], P(None, 'ga'), may hold values from -2 to 2
- send_index: int32 [16, 16, 32], P('ga'), may hold values from -1 to 511, as said below
- recv_index: int32 [8192], P('ga'), may hold values from -1 to 511, as said below
- dmat: float32 [192, 13, 13], replicated, may hold values from -0.5 to 4, as said below
- displaced: int32 [256], P('pert'), parts along dimension 0, may hold values from 0 to 191, as said below
- mode: float32 [3, 256], P(None, 'pert'), parts along dimension 1, may hold values from -5 to 5
Outputs:
- dvpsi: bfloat16 [4, 8192, 256], P('pert', 'ga'), parts along dimension 0
There are 2 independent parts, one for each index of `pert`. A program takes and returns all parts, laid end to end along the dimension named above; an argument that names none is the same for every part. Nothing has to cross between parts.
Inputs may be any that keep to these rules, and one draw needn't show every extreme that they name: `send_index`: entry [s, d, c] is a row of device s's k-sphere block in local numbering, or -1 for an unused slot; the rows device s sends are distinct; in every draw some device receives 32 rows from every device. `recv_index`: entry r is s * 32 + c, naming slot c from device s among the rows received by the device of row r, or -1 for a row with no k-sphere counterpart; every used slot is named by exactly one row of its receiving device and no unused slot is named. `dmat`: each atom's block is symmetric. `displaced`: 128 distinct atoms.
All inputs are finite; a program needn't handle non-finite values.
Results may differ from a plain program's by a relative error of at most 0.0057.
Values may be sent and summed in bfloat16 or wider, within the bound.
A program may use at most 128 MiB of HBM per device.

v0:
```python
import functools

import jax
import jax.numpy as jnp
from jax import lax
from jax.experimental import pallas as pl
from jax.experimental.pallas import tpu as pltpu
from jax.sharding import PartitionSpec as P

LANES = 128
RING = 4
CORE_Y = 4
BF16 = jnp.bfloat16
F32 = jnp.float32
VMEM_LIMIT = 56 * 1024 * 1024


def round_up(value, step):
    return -(-value // step) * step


def dot(a, b):
    return jnp.dot(a, b, preferred_element_type=F32)


def dot_t(a, b):
    return lax.dot_general(a, b, (((0,), (0,)), ((), ())), preferred_element_type=F32)


def pack_kernel(slot_ref, psi_ref, out_ref):
    rows = psi_ref.shape[1]
    bands = psi_ref.shape[2]
    slots = slot_ref.shape[1]
    pick = (lax.broadcasted_iota(jnp.int32, (rows, slots), 0) == slot_ref[...]).astype(BF16)
    for part in range(2):
        out_ref[:, part * bands:(part + 1) * bands] = dot_t(pick, psi_ref[part]).astype(BF16)


def pack_rows(slots, psi_k):
    return pl.pallas_call(
        pack_kernel,
        out_shape=jax.ShapeDtypeStruct((slots.shape[1], 2 * psi_k.shape[2]), BF16),
        compiler_params=pltpu.CompilerParams(vmem_limit_bytes=VMEM_LIMIT),
    )(slots, psi_k)


class Layout:
    def __init__(self, groups, atoms, per_atom, total):
        self.groups = groups
        self.blocks = groups // CORE_Y
        self.gang = CORE_Y
        if self.blocks != RING:
            self.blocks = RING
            self.gang = groups // RING
        self.per_shard = atoms // groups
        self.per_atom = per_atom
        self.used = self.per_shard * per_atom
        self.rows = round_up(self.used, 16)
        self.block = self.gang * self.rows
        self.padded = round_up(self.block, LANES)
        self.total = total
        slack = total - atoms * per_atom
        self.window = min(total, round_up(self.gang * self.used + slack + 16, LANES))
        self.starts = [
            min(b * self.gang * self.used // 16 * 16, total - self.window) for b in range(self.blocks)
        ]


def columns_of(layout, info_ref, b):
    wide = info_ref[:, b * layout.padded:(b + 1) * layout.padded]
    return jnp.transpose(wide)[: layout.block]


def select(layout, beta_ref, info, b):
    start = layout.starts[b]
    ids = lax.broadcasted_iota(jnp.int32, (layout.block, layout.window), 1) + start
    pick = (ids == info[:, 0:1].astype(jnp.int32)).astype(BF16)
    rows = pl.ds(start, layout.window)
    return dot(pick, beta_ref[0, rows, :]), dot(pick, beta_ref[1, rows, :])


def row_scale(g_ref, info):
    total = info[:, 1:2] * g_ref[0:1, :]
    for x in range(1, g_ref.shape[0]):
        total = total + info[:, x + 1:x + 2] * g_ref[x:x + 1, :]
    return total


def regroup(arrived_ref, slot_ref, wave):
    slots, rows = arrived_ref.shape[0], wave.shape[0]
    pick = (lax.broadcasted_iota(jnp.int32, (slots, rows), 0) == slot_ref[...]).astype(BF16)
    wave[...] = dot_t(pick, arrived_ref[...]).astype(BF16)


def project_block(layout, beta_ref, info_ref, g_ref, wave, store, b):
    bands = wave.shape[1] // 2
    info = columns_of(layout, info_ref, b)
    real, imag = select(layout, beta_ref, info, b)
    scale = row_scale(g_ref, info)
    stacked = wave[...]
    x = dot(real.astype(BF16), stacked)
    y = dot(imag.astype(BF16), stacked)
    store(0, (x[:, :bands] + y[:, bands:]).astype(BF16))
    store(1, (x[:, bands:] - y[:, :bands]).astype(BF16))
    x = dot((scale * imag).astype(BF16), stacked)
    y = dot((scale * real).astype(BF16), stacked)
    store(2, (x[:, :bands] - y[:, bands:]).astype(BF16))
    store(3, (x[:, bands:] + y[:, :bands]).astype(BF16))


def prepare_block(layout, beta_ref, info_ref, g_ref, left_ref, b):
    info = columns_of(layout, info_ref, b)
    real, imag = select(layout, beta_ref, info, b)
    scale = row_scale(g_ref, info)
    for k, term in enumerate((scale * imag, -scale * real, real, imag)):
        left_ref[b, k] = term.astype(BF16).T


def back_block(left_ref, b, coupled):
    width = coupled.shape[1] // 2
    bands = width // 2
    first, second = coupled[:, :width], coupled[:, width:]
    x = dot(left_ref[b, 0], first) + dot(left_ref[b, 2], second)
    y = dot(left_ref[b, 1], first) + dot(left_ref[b, 3], second)
    return x[:, :bands] - y[:, bands:], x[:, bands:] + y[:, :bands]


def project_kernel(layout, arrived_ref, slot_ref, beta_ref, info_ref, g_ref, out_ref, wave):
    regroup(arrived_ref, slot_ref, wave)
    bands = wave.shape[1] // 2
    for b in range(layout.blocks):

        def store(k, value, b=b):
            out_ref[b * layout.block:(b + 1) * layout.block, k * bands:(k + 1) * bands] = value

        project_block(layout, beta_ref, info_ref, g_ref, wave, store, b)


def finish_kernel(layout, beta_ref, info_ref, g_ref, coupled_ref, out_ref, left, total):
    for b in range(layout.blocks):
        prepare_block(layout, beta_ref, info_ref, g_ref, left, b)
        parts = back_block(left, b, coupled_ref[b * layout.block:(b + 1) * layout.block, :])
        for k in range(2):
            total[k] = parts[k] if b == 0 else total[k] + parts[k]
    out_ref[...] = total[...].astype(BF16)


def params(**extra):
    return pltpu.CompilerParams(vmem_limit_bytes=VMEM_LIMIT, **extra)


def separate_steps(layout, arrived, slots, beta_k, beta_kq, info, g_k, g_kq, coupling):
    rows, width = slots.shape[1], arrived.shape[1]
    terms = pl.pallas_call(
        functools.partial(project_kernel, layout),
        out_shape=jax.ShapeDtypeStruct((layout.groups * layout.rows, 2 * width), BF16),
        scratch_shapes=[pltpu.VMEM((rows, width), BF16)],
        compiler_params=params(),
    )(arrived, slots, beta_k, info, g_k)
    shard = lax.psum_scatter(terms.astype(F32), "ga", scatter_dimension=0, tiled=True)
    mixed = jnp.dot(
        coupling, shard, precision=lax.Precision.HIGHEST, preferred_element_type=F32
    ).astype(BF16)
    coupled = lax.all_gather(mixed, "ga", axis=0, tiled=True)
    return pl.pallas_call(
        functools.partial(finish_kernel, layout),
        out_shape=jax.ShapeDtypeStruct((2, rows, width // 2), BF16),
        scratch_shapes=[
            pltpu.VMEM((layout.blocks, 4, rows, layout.block), BF16),
            pltpu.VMEM((2, rows, width // 2), F32),
        ],
        compiler_params=params(),
    )(beta_kq, info, g_kq, coupled)


class Sends:
    def __init__(self, send_sem, recv_sem):
        self.send_sem, self.recv_sem = send_sem, recv_sem
        self.started = []

    def start(self, source, target, device):
        k = len(self.started)
        copy = pltpu.make_async_remote_copy(
            src_ref=source,
            dst_ref=target,
            send_sem=self.send_sem.at[k],
            recv_sem=self.recv_sem.at[k],
            device_id={"ga": device},
            device_id_type=pl.DeviceIdType.MESH,
        )
        copy.start()
        self.started.append(copy)
        return copy

    def finish(self):
        for copy in self.started:
            copy.wait_send()


def fused_kernel(
    layout, arrived_ref, slot_ref, beta_k_ref, info_ref, g_k_ref, g_kq_ref, coupling_ref, beta_kq_hbm,
    out_ref, wave, part, core_in, mine, y_in, y_sum, za_in, za_mid, zb_in, zb_mid, b_sum, b_in,
    coupled, left, total, beta_kq, send_sem, recv_sem, load_sem,
):
    me = lax.axis_index("ga")
    c, y, z = me % 2, (me // 2) % 2, me // 4

    def index(zz, yy, cc):
        return (zz * 2 + yy) * 2 + cc

    up, down, far = (z + 1) % RING, (z + RING - 1) % RING, (z + 2) % RING
    other_core, other_y = index(z, y, 1 - c), index(z, 1 - y, c)
    next_z, last_z = index(up, y, c), index(down, y, c)
    load = pltpu.make_async_copy(beta_kq_hbm, beta_kq, load_sem)
    load.start()

    barrier = pltpu.get_barrier_semaphore()
    partners = (other_core, other_y, next_z, last_z)
    for partner in partners:
        pl.semaphore_signal(barrier, inc=1, device_id={"ga": partner}, device_id_type=pl.DeviceIdType.MESH)
    pl.semaphore_wait(barrier, len(partners))

    sends = Sends(send_sem, recv_sem)
    rows = layout.rows
    bands = wave.shape[1] // 2
    half = 2 * bands
    low, high = pl.ds(0, half), pl.ds(half, half)
    left_cols, right_cols = pl.ds(0, bands), pl.ds(bands, bands)
    high_left, high_right = pl.ds(half, bands), pl.ds(half + bands, bands)

    def add(first, *others):
        value = first.astype(F32)
        for other in others:
            value = value + other.astype(F32)
        return value

    regroup(arrived_ref, slot_ref, wave)
    core_copies = []
    for b in range(RING):

        def store(k, value, b=b):
            for yy in range(2):
                for cc in range(2):
                    at = (yy * 2 + cc) * rows
                    part[b, yy, cc, :, k * bands:(k + 1) * bands] = value[at:at + rows]

        project_block(layout, beta_k_ref, info_ref, g_k_ref, wave, store, b)
        core_copies.append([
            sends.start(part.at[b, yy, 1 - c], core_in.at[b, yy], other_core) for yy in range(2)
        ])
    for b in range(RING):
        for yy in range(2):
            core_copies[b][yy].wait_recv()
            mine[b, yy] = add(part[b, yy, c], core_in[b, yy]).astype(BF16)

    zb_up = sends.start(mine.at[far, :, :, high_left], zb_in.at[0], next_z)
    zb_down = sends.start(mine.at[far, :, :, high_right], zb_in.at[1], last_z)
    y_copies = [sends.start(mine.at[b, 1 - y, :, low], y_in.at[b], other_y) for b in range(RING)]
    zb_up_own = sends.start(mine.at[up, :, :, high_right], zb_in.at[2], next_z)
    zb_down_own = sends.start(mine.at[down, :, :, high_left], zb_in.at[3], last_z)

    load.wait()
    prepare_block(layout, beta_kq, info_ref, g_kq_ref, left, 0)
    prepare_block(layout, beta_kq, info_ref, g_kq_ref, left, 1)
    zb_up.wait_recv()
    zb_mid[0] = add(mine[up, :, :, half:half + bands], zb_in[0]).astype(BF16)
    zb_up_sum = sends.start(zb_mid.at[0], zb_in.at[4], next_z)
    zb_down.wait_recv()
    zb_mid[1] = add(mine[down, :, :, half + bands:], zb_in[1]).astype(BF16)
    zb_down_sum = sends.start(zb_mid.at[1], zb_in.at[5], last_z)

    for b in range(RING):
        y_copies[b].wait_recv()
        y_sum[b] = add(mine[b, y, :, :half], y_in[b]).astype(BF16)
    za_up = sends.start(y_sum.at[far, :, left_cols], za_in.at[0], next_z)
    za_down = sends.start(y_sum.at[far, :, right_cols], za_in.at[1], last_z)
    za_up_own = sends.start(y_sum.at[up, :, right_cols], za_in.at[2], next_z)
    za_down_own = sends.start(y_sum.at[down, :, left_cols], za_in.at[3], last_z)

    prepare_block(layout, beta_kq, info_ref, g_kq_ref, left, 2)
    for copy in (zb_up_own, zb_down_own, zb_up_sum, zb_down_sum):
        copy.wait_recv()
    b_sum[:, :, :bands] = add(mine[z, :, :, half:half + bands], zb_in[4], zb_in[3]).astype(BF16)
    b_sum[:, :, bands:] = add(mine[z, :, :, half + bands:], zb_in[5], zb_in[2]).astype(BF16)
    b_y = sends.start(b_sum.at[1 - y], b_in, other_y)

    za_up.wait_recv()
    za_mid[0] = add(y_sum[up, :, :bands], za_in[0]).astype(BF16)
    za_up_sum = sends.start(za_mid.at[0], za_in.at[4], next_z)
    za_down.wait_recv()
    za_mid[1] = add(y_sum[down, :, bands:], za_in[1]).astype(BF16)
    za_down_sum = sends.start(za_mid.at[1], za_in.at[5], last_z)

    prepare_block(layout, beta_kq, info_ref, g_kq_ref, left, 3)

    def couple(value):
        return jnp.dot(
            coupling_ref[...], value, precision=lax.Precision.HIGHEST, preferred_element_type=F32
        ).astype(BF16)

    b_y.wait_recv()
    coupled[z, y, c, :, half:] = couple(add(b_sum[y], b_in[...]))
    own = coupled.at[z, y, c, :, high]
    gb_y = sends.start(own, own, other_y)
    for copy in (za_up_own, za_down_own, za_up_sum, za_down_sum):
        copy.wait_recv()
    coupled[z, y, c, :, :bands] = couple(add(y_sum[z, :, :bands], za_in[4], za_in[3]))
    coupled[z, y, c, :, bands:half] = couple(add(y_sum[z, :, bands:], za_in[5], za_in[2]))

    own = coupled.at[z, y, c, :, low]
    ga_up = sends.start(own, own, next_z)
    ga_down = sends.start(own, own, last_z)
    ga_y = [sends.start(own, own, other_y)]
    gc = [sends.start(coupled.at[z, y, c], coupled.at[z, y, c], other_core)]
    gb_y.wait_recv()
    pair = coupled.at[z, :, c, :, high]
    gb_up = sends.start(pair, pair, next_z)
    gb_down = sends.start(pair, pair, last_z)

    def forward(ref, device):
        return sends.start(ref, ref, device)

    ga_up.wait_recv()
    from_down_a = coupled.at[down, y, c, :, low]
    ga_up2 = forward(coupled.at[down, y, c, :, left_cols], next_z)
    ga_y.append(forward(from_down_a, other_y))
    ga_down.wait_recv()
    from_up_a = coupled.at[up, y, c, :, low]
    ga_down2 = forward(coupled.at[up, y, c, :, right_cols], last_z)
    ga_y.append(forward(from_up_a, other_y))
    ga_y[0].wait_recv()
    gc.append(forward(coupled.at[z, 1 - y, c], other_core))

    gb_up.wait_recv()
    gb_up2 = forward(coupled.at[down, :, c, :, high_left], next_z)
    gc_down = forward(coupled.at[down, :, c, :, high], other_core)
    gb_down.wait_recv()
    gb_down2 = forward(coupled.at[up, :, c, :, high_right], last_z)
    gc_up = forward(coupled.at[up, :, c, :, high], other_core)

    def back(b, first):
        parts = back_block(left, b, coupled[b].reshape(layout.block, 2 * half))
        for k in range(2):
            total[k] = parts[k] if first else total[k] + parts[k]

    for copy in gc:
        copy.wait_recv()
    back(z, True)

    ga_up2.wait_recv()
    ga_down2.wait_recv()
    ga_y.append(forward(coupled.at[far, y, c, :, low], other_y))
    ga_y[1].wait_recv()
    gc_down_a = forward(coupled.at[down, :, c, :, low], other_core)
    ga_y[2].wait_recv()
    gc_up_a = forward(coupled.at[up, :, c, :, low], other_core)
    gc_down.wait_recv()
    gc_down_a.wait_recv()
    back(down, False)
    gb_up2.wait_recv()
    gb_down2.wait_recv()
    gc_far = forward(coupled.at[far, :, c, :, high], other_core)
    ga_y[3].wait_recv()
    gc_far_a = forward(coupled.at[far, :, c, :, low], other_core)
    gc_up.wait_recv()
    gc_up_a.wait_recv()
    back(up, False)
    gc_far.wait_recv()
    gc_far_a.wait_recv()
    parts = back_block(left, far, coupled[far].reshape(layout.block, 2 * half))
    for k in range(2):
        out_ref[k] = (total[k] + parts[k]).astype(BF16)
    sends.finish()


COPIES = 64


def fused(layout, arrived, slots, beta_k, beta_kq, info, g_k, g_kq, coupling):
    rows, width = slots.shape[1], arrived.shape[1]
    bands = width // 2
    r = layout.rows
    vmem = pl.BlockSpec(memory_space=pltpu.VMEM)

    def buffer(*shape, dtype=BF16):
        return pltpu.VMEM(shape, dtype)

    return pl.pallas_call(
        functools.partial(fused_kernel, layout),
        in_specs=[vmem] * 7 + [pl.BlockSpec(memory_space=pl.ANY)],
        out_specs=vmem,
        out_shape=jax.ShapeDtypeStruct((2, rows, bands), BF16),
        scratch_shapes=[
            buffer(rows, width),
            buffer(RING, 2, 2, r, 2 * width),
            buffer(RING, 2, r, 2 * width),
            buffer(RING, 2, r, 2 * width),
            buffer(RING, r, width),
            buffer(RING, r, width),
            buffer(6, r, bands),
            buffer(2, r, bands),
            buffer(6, 2, r, bands),
            buffer(2, 2, r, bands),
            buffer(2, r, width),
            buffer(r, width),
            buffer(RING, 2, 2, r, 2 * width),
            buffer(RING, 4, rows, layout.block),
            buffer(2, rows, bands, dtype=F32),
            pltpu.VMEM(beta_kq.shape, BF16),
            pltpu.SemaphoreType.DMA((COPIES,)),
            pltpu.SemaphoreType.DMA((COPIES,)),
            pltpu.SemaphoreType.DMA,
        ],
        compiler_params=params(collective_id=0, has_side_effects=True),
    )(arrived, slots, beta_k, info, g_k, g_kq, coupling, beta_kq)


def pad_rows(layout, values, fill):
    k = values.shape[0]
    parts = values.reshape(k, layout.groups, layout.used)
    parts = jnp.pad(parts, ((0, 0), (0, 0), (0, layout.rows - layout.used)), constant_values=fill)
    parts = parts.reshape(k, layout.blocks, layout.block)
    parts = jnp.pad(parts, ((0, 0), (0, 0), (0, layout.padded - layout.block)), constant_values=fill)
    return parts.reshape(k, layout.blocks * layout.padded)


def block_coupling(layout, dmat, atoms):
    mine = lax.dynamic_slice_in_dim(atoms, lax.axis_index("ga") * layout.per_shard, layout.per_shard)
    blocks = jnp.take(dmat, mine, axis=0)
    eye = jnp.eye(layout.per_shard, dtype=F32)
    full = (blocks[:, :, None, :] * eye[:, None, :, None]).reshape(layout.used, layout.used)
    extra = layout.rows - layout.used
    return jnp.pad(full, ((0, extra), (0, extra)))


def on_device(psi_k, beta_k, beta_kq, g_k, g_kq, send_index, recv_index, dmat, displaced, mode):
    groups = lax.axis_size("ga")
    total = beta_k.shape[2]
    rows = beta_k.shape[1]
    per_atom = dmat.shape[1]
    layout = Layout(groups, displaced.shape[0], per_atom, total)

    packed = pack_rows(send_index.reshape(1, -1), psi_k)
    arrived = lax.all_to_all(packed, "ga", split_axis=0, concat_axis=0, tiled=True)

    rank = jnp.sum((displaced[None, :] < displaced[:, None]).astype(jnp.int32), axis=1)
    place = rank[None, :] == jnp.arange(displaced.shape[0], dtype=jnp.int32)[:, None]
    atoms = jnp.sum(jnp.where(place, displaced[None, :], 0), axis=1)
    moves = jnp.sum(jnp.where(place[None], mode[:, None, :], 0.0), axis=2)
    steps = jnp.tile(jnp.arange(per_atom, dtype=F32), displaced.shape[0])
    source = jnp.repeat(atoms.astype(F32) * per_atom, per_atom) + steps
    source = pad_rows(layout, source[None], -1.0)
    weights = pad_rows(layout, jnp.repeat(moves, per_atom, axis=1), 0.0)
    filler = jnp.zeros((8 - 1 - weights.shape[0], source.shape[1]), F32)
    info = jnp.concatenate([source, weights, filler], axis=0)
    coupling = block_coupling(layout, dmat, atoms)
    run = fused if groups == RING * CORE_Y else separate_steps
    return run(
        layout, arrived, recv_index.reshape(1, -1), jnp.transpose(beta_k, (0, 2, 1)),
        jnp.transpose(beta_kq, (0, 2, 1)), info, g_k, g_kq, coupling,
    )


def solution(mesh):
    in_specs = (
        P(None, "ga", None),
        P(None, "ga", None),
        P(None, "ga", None),
        P(None, "ga"),
        P(None, "ga"),
        P("ga", None, None),
        P("ga"),
        P(),
        P("pert"),
        P(None, "pert"),
    )
    out_specs = P("pert", "ga", None)
    return jax.shard_map(
        on_device, mesh=mesh, in_specs=in_specs, out_specs=out_specs, check_vma=False
    )
```

profile of v0, /device:TPU:0, one launch (start us, length us, event | category | flops | bytes accessed | tf_op | source)
XLA Modules:
  0.0 98.9 jit_solution(17444447022678795055)
XLA Ops:
  0.0 0.0 copy-start.1
  0.0 1.4 %reshape.105.slot_ref = s32[1,512]{1,0:T(1,128)} reshape(s32[1,16,32]{2,1,0:T(8,128)} %param.15) | data formatting | bytes 4096 | tf_op jit(solution)/shard_map/reshape | solution.py:443
  1.4 2.3 %shard_map.100 = bf16[512,512]{1,0:T(8,128)(2,1)} custom-call(s32[1,512]{1,0:T(1,128)} %reshape.105.slot_ref, bf16[2,512,256]{2,1,0:T(8,128)(2,1)} %psi_ref.1), custom_call_target="tpu_custom_call" | custom-call | tf_op jit(solution)/shard_map/pallas_call | solution.py:40
  3.7 7.4 %all-to-all-start = ((bf16[16,32,512]{2,1,0:T(8,128)(2,1)}), bf16[16,32,512]{2,1,0:T(8,128)(2,1)S(1)}, u32[]{:S(2)}, u32[]{:S(2)}) async-start(bf16[16,32,512]{2,1,0:T(8,128)(2,1)} %bitcast.15), calls=%async_computation | async-start | bytes 1048576 | tf_op jit(solution)/shard_map/all_to_all | solution.py:444
  11.1 0.9 convert_reduce_fusion
  12.0 0.8 select_reduce_fusion.1
  12.8 0.1 compare_and_fusion
  12.9 1.8 %copy.13 = f32[192,13,13]{2,1,0:T(8,128)S(1)} copy(f32[192,13,13]{0,2,1:T(8,128)} %param.17) | data formatting | bytes 259584 | tf_op args[7]
  14.7 0.6 gather_fusion
  15.3 0.1 broadcast_select_fusion
  15.4 0.1 broadcast_multiply_fusion
  15.5 0.2 mul.37
  15.6 0.1 mul.32
  15.7 0.1 broadcast_in_dim.63
  15.8 0.1 broadcast_in_dim.64
  15.9 0.1 tile.12
  16.0 0.1 reshape.107
  16.1 0.0 copy-done.1
  16.1 0.1 select_reduce_fusion
  16.3 0.1 broadcast_in_dim.68
  16.4 0.1 reshape_reshape.3
  16.5 0.6 pad.24.coupling_ref
  17.2 0.1 reshape.109
  17.3 0.1 pad.27.clone
  17.4 0.7 maximum_maximum_fusion.info_ref
  18.1 7.3 %all-to-all-done = bf16[16,32,512]{2,1,0:T(8,128)(2,1)S(1)} async-done(((bf16[16,32,512]{2,1,0:T(8,128)(2,1)}), bf16[16,32,512]{2,1,0:T(8,128)(2,1)S(1)}, u32[]{:S(2)}, u32[]{:S(2)}) %all-to-all-start) | async-done | bytes 524320 | tf_op jit(solution)/shard_map/all_to_all | solution.py:444
  25.4 0.0 copy-start
  25.4 0.8 copy-done
  26.2 70.9 %shard_map.101 = bf16[2,512,256]{2,1,0:T(8,128)(2,1)} custom-call(bf16[512,512]{1,0:T(8,128)(2,1)} %bitcast.16, s32[1,512]{1,0:T(1,128)} %bitcast.19, bf16[2,2496,512]{2,1,0:T(8,128)(2,1)} %bitcast.13, f32[8,2048]{1,0:T(8,128)} %maximum_maximum_fusion.info_ref, f32[3,512]{1,0:T(4,128)} %g_k_ref.1, f32[3,512]{1,0:T(4,128)} %g_kq_ref.1, ...), custom_call_target="tpu_custom_call" | custom-call | tf_op jit(solution)/shard_map/pallas_call | solution.py:388
  97.1 1.9 %copy.17 = bf16[2,512,256]{2,1,0:T(8,128)(2,1)} copy(bf16[2,512,256]{2,1,0:T(8,128)(2,1)} %shard_map.101) | data formatting | bytes 1048576
  (13 shorter events, 0.1 us)
Async XLA Ops:
  0.0 16.1 %copy-start.1 = (f32[3,128]{1,0:T(4,128)S(1)}, f32[3,128]{1,0:T(4,128)}, u32[]{:S(2)}) copy-start(f32[3,128]{1,0:T(4,128)} %param.19) | copy-start | bytes 4612
  3.7 21.7 %all-to-all-start = ((bf16[16,32,512]{2,1,0:T(8,128)(2,1)}), bf16[16,32,512]{2,1,0:T(8,128)(2,1)S(1)}, u32[]{:S(2)}, u32[]{:S(2)}) async-start(bf16[16,32,512]{2,1,0:T(8,128)(2,1)} %bitcast.15), calls=%async_computation | async-start | bytes 1048576 | tf_op jit(solution)/shard_map/all_to_all | solution.py:444
  25.4 0.8 copy-start
where the time goes:
time: 99.3 us; the launch traced here: 98.9 us
  Pallas kernels  73.2 us (74%)
  local copies, waits for them, and re-layouts  8.04 us (8%)
  starting transfers between devices  7.41 us (7%)
  waiting for transfers between devices  7.32 us (7%)
  other arithmetic  2.8 us (3%)
    pallas_call x1, Pallas kernels, fused(): pl.pallas_call(functools.partial(fused_kernel, layout), in_specs=[vmem] *...  70.9 us
    all_to_all x1, starting transfers between devices, on_device(): lax.all_to_all(packed, 'ga', split_axis=0, concat_axis=0, tiled=True)  7.41 us
    all_to_all x1, waiting for transfers between devices, on_device(): lax.all_to_all(packed, 'ga', split_axis=0, concat_axis=0, tiled=True)  7.32 us
    unnamed x10, local copies, waits for them, and re-layouts  4.5 us
    pallas_call x1, Pallas kernels, pack_rows(): pl.pallas_call(pack_kernel, out_shape=jax.ShapeDtypeStruct((slots.shape[1...  2.31 us
  transfers between devices with their start and end apart: 1, of which 1 were waited for; matrix products, arithmetic and copies ran while one was open for 7% of the time, Pallas kernels for 0%

commit v1 on v0

--- a/solution.py
+++ b/solution.py
@@ -2,6 +2,7 @@
 
 import jax
 import jax.numpy as jnp
+import numpy as np
 from jax import lax
 from jax.experimental import pallas as pl
 from jax.experimental.pallas import tpu as pltpu
@@ -92,27 +93,27 @@
     wave[...] = dot_t(pick, arrived_ref[...]).astype(BF16)
 
 
-def project_block(layout, beta_ref, info_ref, g_ref, wave, store, b):
-    bands = wave.shape[1] // 2
-    info = columns_of(layout, info_ref, b)
+def selected_terms(layout, beta_ref, info, g_ref, b):
     real, imag = select(layout, beta_ref, info, b)
     scale = row_scale(g_ref, info)
-    stacked = wave[...]
-    x = dot(real.astype(BF16), stacked)
-    y = dot(imag.astype(BF16), stacked)
+    return real, imag, scale * imag, scale * real
+
+
+def project_block(terms, stacked, store):
+    bands = stacked.shape[1] // 2
+    x = dot(terms[0], stacked)
+    y = dot(terms[1], stacked)
     store(0, (x[:, :bands] + y[:, bands:]).astype(BF16))
     store(1, (x[:, bands:] - y[:, :bands]).astype(BF16))
-    x = dot((scale * imag).astype(BF16), stacked)
-    y = dot((scale * real).astype(BF16), stacked)
+    x = dot(terms[2], stacked)
+    y = dot(terms[3], stacked)
     store(2, (x[:, :bands] - y[:, bands:]).astype(BF16))
     store(3, (x[:, bands:] + y[:, :bands]).astype(BF16))
 
 
-def prepare_block(layout, beta_ref, info_ref, g_ref, left_ref, b):
-    info = columns_of(layout, info_ref, b)
-    real, imag = select(layout, beta_ref, info, b)
-    scale = row_scale(g_ref, info)
-    for k, term in enumerate((scale * imag, -scale * real, real, imag)):
+def prepare_block(layout, beta_ref, info, g_ref, left_ref, b):
+    real, imag, slope_real, slope_imag = selected_terms(layout, beta_ref, info, g_ref, b)
+    for k, term in enumerate((slope_real, -slope_imag, real, imag)):
         left_ref[b, k] = term.astype(BF16).T
 
 
@@ -133,12 +134,14 @@
         def store(k, value, b=b):
             out_ref[b * layout.block:(b + 1) * layout.block, k * bands:(k + 1) * bands] = value
 
-        project_block(layout, beta_ref, info_ref, g_ref, wave, store, b)
+        info = columns_of(layout, info_ref, b)
+        terms = [term.astype(BF16) for term in selected_terms(layout, beta_ref, info, g_ref, b)]
+        project_block(terms, wave[...], store)
 
 
 def finish_kernel(layout, beta_ref, info_ref, g_ref, coupled_ref, out_ref, left, total):
     for b in range(layout.blocks):
-        prepare_block(layout, beta_ref, info_ref, g_ref, left, b)
+        prepare_block(layout, beta_ref, columns_of(layout, info_ref, b), g_ref, left, b)
         parts = back_block(left, b, coupled_ref[b * layout.block:(b + 1) * layout.block, :])
         for k in range(2):
             total[k] = parts[k] if b == 0 else total[k] + parts[k]
@@ -197,12 +200,57 @@
             copy.wait_send()
 
 
+def exact_dot(a, b):
+    return jnp.dot(a, b, precision=lax.Precision.HIGHEST, preferred_element_type=F32)
+
+
+def slot_row(send_ref):
+    receivers, cap = send_ref.shape
+    column = lax.broadcasted_iota(jnp.int32, (cap, receivers * cap), 1)
+    inner = lax.broadcasted_iota(jnp.int32, (cap, receivers * cap), 0)
+    wide = exact_dot(send_ref[...].astype(F32), (column % cap == inner).astype(F32))
+    column = lax.broadcasted_iota(jnp.int32, wide.shape, 1)
+    outer = lax.broadcasted_iota(jnp.int32, wide.shape, 0)
+    return jnp.sum(jnp.where(column // cap == outer, wide, 0.0), axis=0, keepdims=True).astype(jnp.int32)
+
+
+def sorted_info(layout, displaced_ref, mode_ref, table_ref, values, info):
+    parts = mode_ref.shape[0]
+    values[...] = jnp.zeros_like(values)
+    values[0:1, :] = displaced_ref[...].astype(F32)
+    values[1:1 + parts, :] = mode_ref[...]
+    by_atom = jnp.transpose(values[...])
+    smaller = (by_atom[:, 0:1] < values[0:1, :]).astype(F32)
+    rank = jnp.sum(smaller, axis=0, keepdims=True)
+    lane = lax.broadcasted_iota(jnp.int32, (layout.block, values.shape[0]), 1)
+    for b in range(layout.blocks):
+        place = columns_of(layout, table_ref, b)
+        found = exact_dot((place[:, 0:1] == rank).astype(F32), by_atom)
+        source = jnp.where(place[:, 0:1] < 0, -1.0, found * layout.per_atom + place[:, 1:2])
+        info[b] = jnp.where(lane == 0, source, jnp.where(lane == 7, found[:, 0:1], found))
+
+
+def coupling_matrix(layout, dmat_ref, atom, proj, spread_ref, same_ref):
+    lanes = lax.broadcasted_iota(jnp.int32, (layout.rows, dmat_ref.shape[2]), 1)
+    pick = (lanes == atom.astype(jnp.int32)).astype(F32)
+    rows = jnp.zeros((layout.rows, layout.per_atom), F32)
+    for i in range(layout.per_atom):
+        found = lax.dot_general(
+            pick, dmat_ref[i], (((1,), (1,)), ((), ())),
+            precision=lax.Precision.HIGHEST, preferred_element_type=F32,
+        )
+        rows = rows + jnp.where(proj == i, found, 0.0)
+    return exact_dot(rows, spread_ref[...]) * same_ref[...]
+
+
 def fused_kernel(
-    layout, arrived_ref, slot_ref, beta_k_ref, info_ref, g_k_ref, g_kq_ref, coupling_ref, beta_kq_hbm,
+    layout, psi_ref, send_ref, slot_ref, displaced_ref, mode_ref, table_ref, g_k_ref, g_kq_ref, dmat_ref,
+    proj_ref, spread_ref, same_ref, beta_k_hbm, beta_kq_hbm,
     out_ref, wave, part, core_in, mine, y_in, y_sum, za_in, za_mid, zb_in, zb_mid, b_sum, b_in,
-    coupled, left, total, beta_kq, send_sem, recv_sem, load_sem,
+    coupled, left, total, beta_kq, beta_k, packed, arrived, terms, values, info, send_sem, recv_sem, load_sem,
 ):
     me = lax.axis_index("ga")
+    n = layout.groups
     c, y, z = me % 2, (me // 2) % 2, me // 4
 
     def index(zz, yy, cc):
@@ -211,14 +259,23 @@
     up, down, far = (z + 1) % RING, (z + RING - 1) % RING, (z + 2) % RING
     other_core, other_y = index(z, y, 1 - c), index(z, 1 - y, c)
     next_z, last_z = index(up, y, c), index(down, y, c)
-    load = pltpu.make_async_copy(beta_kq_hbm, beta_kq, load_sem)
+    load_k = pltpu.make_async_copy(beta_k_hbm, beta_k, load_sem.at[0])
+    load_k.start()
+    load = pltpu.make_async_copy(beta_kq_hbm, beta_kq, load_sem.at[1])
     load.start()
 
     barrier = pltpu.get_barrier_semaphore()
-    partners = (other_core, other_y, next_z, last_z)
-    for partner in partners:
-        pl.semaphore_signal(barrier, inc=1, device_id={"ga": partner}, device_id_type=pl.DeviceIdType.MESH)
-    pl.semaphore_wait(barrier, len(partners))
+    for step in range(1, n):
+        pl.semaphore_signal(
+            barrier, inc=1, device_id={"ga": (me + step) % n}, device_id_type=pl.DeviceIdType.MESH
+        )
+    rows_here, slots = psi_ref.shape[1], n * send_ref.shape[1]
+    cap = send_ref.shape[1]
+    pick = (lax.broadcasted_iota(jnp.int32, (rows_here, slots), 0) == slot_row(send_ref)).astype(BF16)
+    for k in range(2):
+        width = psi_ref.shape[2]
+        packed[:, :, k * width:(k + 1) * width] = dot_t(pick, psi_ref[k]).astype(BF16).reshape(n, cap, width)
+    pl.semaphore_wait(barrier, n - 1)
 
     sends = Sends(send_sem, recv_sem)
     rows = layout.rows
@@ -234,7 +291,22 @@
             value = value + other.astype(F32)
         return value
 
-    regroup(arrived_ref, slot_ref, wave)
+    psi_copies = [
+        sends.start(packed.at[(me + step) % n], arrived.at[me], (me + step) % n) for step in far_first(n)
+    ]
+    arrived[me] = packed[me]
+    sorted_info(layout, displaced_ref, mode_ref, table_ref, values, info)
+    load_k.wait()
+    for b in range(RING):
+        for k, term in enumerate(selected_terms(layout, beta_k, info[b], g_k_ref, b)):
+            terms[b, k] = term.astype(BF16)
+    load.wait()
+    prepare_block(layout, beta_kq, info[0], g_kq_ref, left, 0)
+    for copy in psi_copies:
+        copy.wait_recv()
+
+    pick = (lax.broadcasted_iota(jnp.int32, (slots, rows_here), 0) == slot_ref[...]).astype(BF16)
+    wave[...] = dot_t(pick, arrived[...].reshape(slots, 2 * bands)).astype(BF16)
     core_copies = []
     for b in range(RING):
 
@@ -244,7 +316,7 @@
                     at = (yy * 2 + cc) * rows
                     part[b, yy, cc, :, k * bands:(k + 1) * bands] = value[at:at + rows]
 
-        project_block(layout, beta_k_ref, info_ref, g_k_ref, wave, store, b)
+        project_block([terms[b, k] for k in range(4)], wave[...], store)
         core_copies.append([
             sends.start(part.at[b, yy, 1 - c], core_in.at[b, yy], other_core) for yy in range(2)
         ])
@@ -259,9 +331,9 @@
     zb_up_own = sends.start(mine.at[up, :, :, high_right], zb_in.at[2], next_z)
     zb_down_own = sends.start(mine.at[down, :, :, high_left], zb_in.at[3], last_z)
 
-    load.wait()
-    prepare_block(layout, beta_kq, info_ref, g_kq_ref, left, 0)
-    prepare_block(layout, beta_kq, info_ref, g_kq_ref, left, 1)
+    shard_atom = info[z, pl.ds(pl.multiple_of((y * 2 + c) * rows, 8), rows), 7:8]
+    coupling = coupling_matrix(layout, dmat_ref, shard_atom, proj_ref[...], spread_ref, same_ref)
+    prepare_block(layout, beta_kq, info[1], g_kq_ref, left, 1)
     zb_up.wait_recv()
     zb_mid[0] = add(mine[up, :, :, half:half + bands], zb_in[0]).astype(BF16)
     zb_up_sum = sends.start(zb_mid.at[0], zb_in.at[4], next_z)
@@ -277,7 +349,7 @@
     za_up_own = sends.start(y_sum.at[up, :, right_cols], za_in.at[2], next_z)
     za_down_own = sends.start(y_sum.at[down, :, left_cols], za_in.at[3], last_z)
 
-    prepare_block(layout, beta_kq, info_ref, g_kq_ref, left, 2)
+    prepare_block(layout, beta_kq, info[2], g_kq_ref, left, 2)
     for copy in (zb_up_own, zb_down_own, zb_up_sum, zb_down_sum):
         copy.wait_recv()
     b_sum[:, :, :bands] = add(mine[z, :, :, half:half + bands], zb_in[4], zb_in[3]).astype(BF16)
@@ -291,12 +363,10 @@
     za_mid[1] = add(y_sum[down, :, bands:], za_in[1]).astype(BF16)
     za_down_sum = sends.start(za_mid.at[1], za_in.at[5], last_z)
 
-    prepare_block(layout, beta_kq, info_ref, g_kq_ref, left, 3)
+    prepare_block(layout, beta_kq, info[3], g_kq_ref, left, 3)
 
     def couple(value):
-        return jnp.dot(
-            coupling_ref[...], value, precision=lax.Precision.HIGHEST, preferred_element_type=F32
-        ).astype(BF16)
+        return exact_dot(coupling, value).astype(BF16)
 
     b_y.wait_recv()
     coupled[z, y, c, :, half:] = couple(add(b_sum[y], b_in[...]))
@@ -373,12 +443,40 @@
     sends.finish()
 
 
-COPIES = 64
-
-
-def fused(layout, arrived, slots, beta_k, beta_kq, info, g_k, g_kq, coupling):
-    rows, width = slots.shape[1], arrived.shape[1]
-    bands = width // 2
+COPIES = 80
+
+
+def far_first(n):
+    return sorted(range(1, n), key=lambda step: -min(step, n - step))
+
+
+def tables(layout):
+    row = np.arange(layout.rows)
+    valid = row < layout.used
+    slot = np.where(valid, row // layout.per_atom, 0)
+    proj = np.where(valid, row % layout.per_atom, -1)
+    table = np.zeros((8, layout.blocks, layout.padded), np.float32)
+    table[0] = -1.0
+    for b in range(layout.blocks):
+        for k in range(layout.gang):
+            at = slice(k * layout.rows, (k + 1) * layout.rows)
+            table[0, b, at] = np.where(valid, (b * layout.gang + k) * layout.per_shard + slot, -1)
+            table[1, b, at] = np.where(valid, proj, 0)
+    spread = (np.arange(layout.per_atom)[:, None] == proj[None]).astype(np.float32)
+    same = (slot[:, None] == slot[None]) & valid[:, None] & valid[None]
+    return (
+        table.reshape(8, -1),
+        proj[:, None].astype(np.int32),
+        spread,
+        same.astype(np.float32),
+    )
+
+
+def fused(layout, psi_k, send_index, recv_index, beta_k, beta_kq, displaced, mode, g_k, g_kq, dmat):
+    rows, bands = psi_k.shape[1:]
+    width = 2 * bands
+    cap = send_index.shape[2]
+    table, proj, spread, same = (jnp.asarray(value) for value in tables(layout))
     r = layout.rows
     vmem = pl.BlockSpec(memory_space=pltpu.VMEM)
 
@@ -387,7 +485,7 @@
 
     return pl.pallas_call(
         functools.partial(fused_kernel, layout),
-        in_specs=[vmem] * 7 + [pl.BlockSpec(memory_space=pl.ANY)],
+        in_specs=[vmem] * 12 + [pl.BlockSpec(memory_space=pl.ANY)] * 2,
         out_specs=vmem,
         out_shape=jax.ShapeDtypeStruct((2, rows, bands), BF16),
         scratch_shapes=[
@@ -407,12 +505,21 @@
             buffer(RING, 4, rows, layout.block),
             buffer(2, rows, bands, dtype=F32),
             pltpu.VMEM(beta_kq.shape, BF16),
+            pltpu.VMEM(beta_k.shape, BF16),
+            buffer(layout.groups, cap, width),
+            buffer(layout.groups, cap, width),
+            buffer(RING, 4, layout.block, rows),
+            buffer(8, displaced.shape[0], dtype=F32),
+            buffer(RING, layout.block, 8, dtype=F32),
             pltpu.SemaphoreType.DMA((COPIES,)),
             pltpu.SemaphoreType.DMA((COPIES,)),
-            pltpu.SemaphoreType.DMA,
+            pltpu.SemaphoreType.DMA((2,)),
         ],
         compiler_params=params(collective_id=0, has_side_effects=True),
-    )(arrived, slots, beta_k, info, g_k, g_kq, coupling, beta_kq)
+    )(
+        psi_k, send_index[0], recv_index.reshape(1, -1), displaced.reshape(1, -1), mode, table, g_k, g_kq,
+        jnp.transpose(dmat, (1, 2, 0)), proj, spread, same, beta_k, beta_kq,
+    )
 
 
 def pad_rows(layout, values, fill):
@@ -439,6 +546,10 @@
     rows = beta_k.shape[1]
     per_atom = dmat.shape[1]
     layout = Layout(groups, displaced.shape[0], per_atom, total)
+
+    beta_k, beta_kq = jnp.transpose(beta_k, (0, 2, 1)), jnp.transpose(beta_kq, (0, 2, 1))
+    if groups == RING * CORE_Y:
+        return fused(layout, psi_k, send_index, recv_index, beta_k, beta_kq, displaced, mode, g_k, g_kq, dmat)
 
     packed = pack_rows(send_index.reshape(1, -1), psi_k)
     arrived = lax.all_to_all(packed, "ga", split_axis=0, concat_axis=0, tiled=True)
@@ -454,10 +565,8 @@
     filler = jnp.zeros((8 - 1 - weights.shape[0], source.shape[1]), F32)
     info = jnp.concatenate([source, weights, filler], axis=0)
     coupling = block_coupling(layout, dmat, atoms)
-    run = fused if groups == RING * CORE_Y else separate_steps
-    return run(
-        layout, arrived, recv_index.reshape(1, -1), jnp.transpose(beta_k, (0, 2, 1)),
-        jnp.transpose(beta_kq, (0, 2, 1)), info, g_k, g_kq, coupling,
+    return separate_steps(
+        layout, arrived, recv_index.reshape(1, -1), beta_k, beta_kq, info, g_k, g_kq, coupling
     )
 
 

time: 99.3 us -> 81.2 us (0.82)
  starting transfers between devices: 7.41 us -> 0 us
  waiting for transfers between devices: 7.32 us -> 0 us
  local copies, waits for them, and re-layouts: 8.04 us -> 1.87 us
  Pallas kernels: 73.2 us -> 79.2 us
  other arithmetic: 2.8 us -> 0 us
    pallas_call x1, Pallas kernels: 70.9 us -> 79.2 us  [fused(): pl.pallas_call(functools.partial(fused_kernel, layout), in_specs=[vmem] *...]
    all_to_all x1 -> x0, starting transfers between devices: 7.41 us -> none  [on_device(): lax.all_to_all(packed, 'ga', split_axis=0, concat_axis=0, tiled=True)]
    all_to_all x1 -> x0, waiting for transfers between devices: 7.32 us -> none  [on_device(): lax.all_to_all(packed, 'ga', split_axis=0, concat_axis=0, tiled=True)]
    unnamed x10 -> x1, local copies, waits for them, and re-layouts: 4.5 us -> 1.87 us
    pallas_call x1 -> x0, Pallas kernels: 2.31 us -> none  [pack_rows(): pl.pallas_call(pack_kernel, out_shape=jax.ShapeDtypeStruct((slots.shape[1...]
    reduce_sum x3 -> x0, other arithmetic: 1.81 us -> none  [the longest x1 0.9 us: on_device(): jnp.sum((displaced[None, :] < displaced[:, None]).astype(jnp.int32), axis=1)]
    reshape x3 -> x0, local copies, waits for them, and re-layouts: 1.54 us -> none  [the longest x1 1.38 us: on_device(): packed = pack_rows(send_index.reshape(1, -1), psi_k)]
  transfers between devices with their start and end apart: 1 -> 0, of which waited for: 1 -> 0; matrix products, arithmetic and copies ran while one was open for 7% -> 0% of each run, Pallas kernels for 0% -> 0%
where the time goes in v1:
time: 81.2 us; the launch traced here: 81.1 us
  Pallas kernels  79.2 us (98%)
  local copies, waits for them, and re-layouts  1.87 us (2%)
    pallas_call x1, Pallas kernels, fused(): pl.pallas_call(functools.partial(fused_kernel, layout), in_specs=[vmem] *...  79.2 us
    unnamed x1, local copies, waits for them, and re-layouts  1.87 us

profile of v1, /device:TPU:0, one launch (start us, length us, event | category | flops | bytes accessed | tf_op | source)
XLA Modules:
  0.0 81.1 jit_solution(17761734872951840601)
XLA Ops:
  0.0 79.2 %shard_map.136 = bf16[2,512,256]{2,1,0:T(8,128)(2,1)} custom-call(bf16[2,512,256]{2,1,0:T(8,128)(2,1)} %psi_ref.1, s32[16,32]{1,0:T(8,128)} %bitcast.9, s32[1,512]{1,0:T(1,128)} %bitcast.10, s32[1,128]{1,0:T(1,128)} %bitcast.11, f32[3,128]{1,0:T(4,128)} %mode_ref.1, f32[8,2048]{1,0:T(8,128)} %constant.8.clone.table_ref, f32[3,512]{1,0:T(4,128)} %g_k_ref.1, ...), custom_call_target="tpu_custom_call" | custom-call | tf_op jit(solution)/shard_map/pallas_call | solution.py:486
  79.2 1.9 %copy.16 = bf16[2,512,256]{2,1,0:T(8,128)(2,1)} copy(bf16[2,512,256]{2,1,0:T(8,128)(2,1)} %shard_map.136) | data formatting | bytes 1048576

commit v2 on v1

--- a/solution.py
+++ b/solution.py
@@ -307,8 +307,24 @@
 
     pick = (lax.broadcasted_iota(jnp.int32, (slots, rows_here), 0) == slot_ref[...]).astype(BF16)
     wave[...] = dot_t(pick, arrived[...].reshape(slots, 2 * bands)).astype(BF16)
-    core_copies = []
-    for b in range(RING):
+    order = (far, up, down, z)
+    core_copies, y_copies, z_copies = [], [], []
+
+    def settle(i):
+        b = order[i]
+        for yy in range(2):
+            core_copies[i][yy].wait_recv()
+            mine[b, yy] = add(part[b, yy, c], core_in[b, yy]).astype(BF16)
+        if i == 0:
+            z_copies.append(sends.start(mine.at[b, :, :, high_left], zb_in.at[0], next_z))
+            z_copies.append(sends.start(mine.at[b, :, :, high_right], zb_in.at[1], last_z))
+        if i == 1:
+            z_copies.append(sends.start(mine.at[b, :, :, high_right], zb_in.at[2], next_z))
+        if i == 2:
+            z_copies.append(sends.start(mine.at[b, :, :, high_left], zb_in.at[3], last_z))
+        y_copies.append(sends.start(mine.at[b, 1 - y, :, low], y_in.at[b], other_y))
+
+    for i, b in enumerate(order):
 
         def store(k, value, b=b):
             for yy in range(2):
@@ -320,20 +336,18 @@
         core_copies.append([
             sends.start(part.at[b, yy, 1 - c], core_in.at[b, yy], other_core) for yy in range(2)
         ])
-    for b in range(RING):
-        for yy in range(2):
-            core_copies[b][yy].wait_recv()
-            mine[b, yy] = add(part[b, yy, c], core_in[b, yy]).astype(BF16)
-
-    zb_up = sends.start(mine.at[far, :, :, high_left], zb_in.at[0], next_z)
-    zb_down = sends.start(mine.at[far, :, :, high_right], zb_in.at[1], last_z)
-    y_copies = [sends.start(mine.at[b, 1 - y, :, low], y_in.at[b], other_y) for b in range(RING)]
-    zb_up_own = sends.start(mine.at[up, :, :, high_right], zb_in.at[2], next_z)
-    zb_down_own = sends.start(mine.at[down, :, :, high_left], zb_in.at[3], last_z)
+        if i > 0:
+            settle(i - 1)
+    settle(RING - 1)
+    zb_up, zb_down, zb_up_own, zb_down_own = z_copies
+
+    def y_settle(i):
+        b = order[i]
+        y_copies[i].wait_recv()
+        y_sum[b] = add(mine[b, y, :, :half], y_in[b]).astype(BF16)
 
     shard_atom = info[z, pl.ds(pl.multiple_of((y * 2 + c) * rows, 8), rows), 7:8]
     coupling = coupling_matrix(layout, dmat_ref, shard_atom, proj_ref[...], spread_ref, same_ref)
-    prepare_block(layout, beta_kq, info[1], g_kq_ref, left, 1)
     zb_up.wait_recv()
     zb_mid[0] = add(mine[up, :, :, half:half + bands], zb_in[0]).astype(BF16)
     zb_up_sum = sends.start(zb_mid.at[0], zb_in.at[4], next_z)
@@ -341,15 +355,16 @@
     zb_mid[1] = add(mine[down, :, :, half + bands:], zb_in[1]).astype(BF16)
     zb_down_sum = sends.start(zb_mid.at[1], zb_in.at[5], last_z)
 
-    for b in range(RING):
-        y_copies[b].wait_recv()
-        y_sum[b] = add(mine[b, y, :, :half], y_in[b]).astype(BF16)
+    y_settle(0)
     za_up = sends.start(y_sum.at[far, :, left_cols], za_in.at[0], next_z)
     za_down = sends.start(y_sum.at[far, :, right_cols], za_in.at[1], last_z)
+    prepare_block(layout, beta_kq, info[1], g_kq_ref, left, 1)
+    y_settle(1)
     za_up_own = sends.start(y_sum.at[up, :, right_cols], za_in.at[2], next_z)
+    y_settle(2)
     za_down_own = sends.start(y_sum.at[down, :, left_cols], za_in.at[3], last_z)
-
     prepare_block(layout, beta_kq, info[2], g_kq_ref, left, 2)
+
     for copy in (zb_up_own, zb_down_own, zb_up_sum, zb_down_sum):
         copy.wait_recv()
     b_sum[:, :, :bands] = add(mine[z, :, :, half:half + bands], zb_in[4], zb_in[3]).astype(BF16)
@@ -362,6 +377,7 @@
     za_down.wait_recv()
     za_mid[1] = add(y_sum[down, :, bands:], za_in[1]).astype(BF16)
     za_down_sum = sends.start(za_mid.at[1], za_in.at[5], last_z)
+    y_settle(3)
 
     prepare_block(layout, beta_kq, info[3], g_kq_ref, left, 3)
 

time: 81.2 us -> 78.1 us (0.962)
  Pallas kernels: 79.2 us -> 76.1 us
    pallas_call x1, Pallas kernels: 79.2 us -> 76.1 us  [fused(): pl.pallas_call(functools.partial(fused_kernel, layout), in_specs=[vmem] *...]
where the time goes in v2:
time: 78.1 us; the launch traced here: 78 us
  Pallas kernels  76.1 us (97%)
  local copies, waits for them, and re-layouts  1.87 us (2%)
    pallas_call x1, Pallas kernels, fused(): pl.pallas_call(functools.partial(fused_kernel, layout), in_specs=[vmem] *...  76.1 us
    unnamed x1, local copies, waits for them, and re-layouts  1.87 us

profile of v2, /device:TPU:0, one launch (start us, length us, event | category | flops | bytes accessed | tf_op | source)
XLA Modules:
  0.0 78.0 jit_solution(9651422100218940377)
XLA Ops:
  0.0 76.1 %shard_map.136 = bf16[2,512,256]{2,1,0:T(8,128)(2,1)} custom-call(bf16[2,512,256]{2,1,0:T(8,128)(2,1)} %psi_ref.1, s32[16,32]{1,0:T(8,128)} %bitcast.9, s32[1,512]{1,0:T(1,128)} %bitcast.10, s32[1,128]{1,0:T(1,128)} %bitcast.11, f32[3,128]{1,0:T(4,128)} %mode_ref.1, f32[8,2048]{1,0:T(8,128)} %constant.8.clone.table_ref, f32[3,512]{1,0:T(4,128)} %g_k_ref.1, ...), custom_call_target="tpu_custom_call" | custom-call | tf_op jit(solution)/shard_map/pallas_call | solution.py:502
  76.1 1.9 %copy.16 = bf16[2,512,256]{2,1,0:T(8,128)(2,1)} copy(bf16[2,512,256]{2,1,0:T(8,128)(2,1)} %shard_map.136) | data formatting | bytes 1048576

commit v3 on v2

--- a/solution.py
+++ b/solution.py
@@ -302,6 +302,9 @@
             terms[b, k] = term.astype(BF16)
     load.wait()
     prepare_block(layout, beta_kq, info[0], g_kq_ref, left, 0)
+    prepare_block(layout, beta_kq, info[1], g_kq_ref, left, 1)
+    shard_atom = info[z, pl.ds(pl.multiple_of((y * 2 + c) * rows, 8), rows), 7:8]
+    coupling = coupling_matrix(layout, dmat_ref, shard_atom, proj_ref[...], spread_ref, same_ref)
     for copy in psi_copies:
         copy.wait_recv()
 
@@ -346,8 +349,6 @@
         y_copies[i].wait_recv()
         y_sum[b] = add(mine[b, y, :, :half], y_in[b]).astype(BF16)
 
-    shard_atom = info[z, pl.ds(pl.multiple_of((y * 2 + c) * rows, 8), rows), 7:8]
-    coupling = coupling_matrix(layout, dmat_ref, shard_atom, proj_ref[...], spread_ref, same_ref)
     zb_up.wait_recv()
     zb_mid[0] = add(mine[up, :, :, half:half + bands], zb_in[0]).astype(BF16)
     zb_up_sum = sends.start(zb_mid.at[0], zb_in.at[4], next_z)
@@ -358,7 +359,6 @@
     y_settle(0)
     za_up = sends.start(y_sum.at[far, :, left_cols], za_in.at[0], next_z)
     za_down = sends.start(y_sum.at[far, :, right_cols], za_in.at[1], last_z)
-    prepare_block(layout, beta_kq, info[1], g_kq_ref, left, 1)
     y_settle(1)
     za_up_own = sends.start(y_sum.at[up, :, right_cols], za_in.at[2], next_z)
     y_settle(2)

time: 78.1 us -> 78.4 us (level)
  no operation moved by 1% of the time
where the time goes in v3:
time: 78.4 us; the launch traced here: 78.2 us
  Pallas kernels  76.3 us (97%)
  local copies, waits for them, and re-layouts  1.87 us (2%)
    pallas_call x1, Pallas kernels, fused(): pl.pallas_call(functools.partial(fused_kernel, layout), in_specs=[vmem] *...  76.3 us
    unnamed x1, local copies, waits for them, and re-layouts  1.87 us

profile of v3, /device:TPU:0, one launch (start us, length us, event | category | flops | bytes accessed | tf_op | source)
XLA Modules:
  0.0 78.2 jit_solution(8021180486150717793)
XLA Ops:
  0.0 76.3 %shard_map.136 = bf16[2,512,256]{2,1,0:T(8,128)(2,1)} custom-call(bf16[2,512,256]{2,1,0:T(8,128)(2,1)} %psi_ref.1, s32[16,32]{1,0:T(8,128)} %bitcast.9, s32[1,512]{1,0:T(1,128)} %bitcast.10, s32[1,128]{1,0:T(1,128)} %bitcast.11, f32[3,128]{1,0:T(4,128)} %mode_ref.1, f32[8,2048]{1,0:T(8,128)} %constant.8.clone.table_ref, f32[3,512]{1,0:T(4,128)} %g_k_ref.1, ...), custom_call_target="tpu_custom_call" | custom-call | tf_op jit(solution)/shard_map/pallas_call | solution.py:502
  76.3 1.9 %copy.16 = bf16[2,512,256]{2,1,0:T(8,128)(2,1)} copy(bf16[2,512,256]{2,1,0:T(8,128)(2,1)} %shard_map.136) | data formatting | bytes 1048576
